TPU v7x, 32 devices: a whole 2x2x4 slice. The times are simulated.
32 devices in a mesh: chan: 4 (over x, core), slab: 8 (over z, y).
Axes of the slice: x: 2, y: 2, z: 4, core: 2. Of those that a mesh axis runs over, the one named last changes fastest.
Arguments:
- beam_images: float32 [64, 512, 4096], P('chan', 'slab'), may hold values from -24 to 24
- chan_weights: int32 [64], P('chan'), may hold values from 1 to 8
- freq_offsets: float32 [64], P('chan'), may hold values from -1 to 1
- half_widths: int32 [5], replicated, may hold values from 16 to 32, as said below
Outputs:
- smoothed: float32 [5, 512, 4096], P(None, 'slab', 'chan')
Inputs may be any that keep to these rules, and one draw needn't show every extreme that they name: `half_widths`: each half-width is at least 16 and at most 32; at least one equals 32.
All inputs are finite; a program needn't handle non-finite values.
Results may differ from a plain program's by a relative error of at most 0.00008.
Values sent between devices are 32-bit elements; how exact they have to be, the bound alone decides.
A program may use at most 128 MiB of HBM per device.

v0:
```python
import jax
import jax.numpy as jnp
from jax import lax
from jax.sharding import PartitionSpec as P

MOMENTS = 5
HW_MAX = 32


def padded(cells, sides, width):
    for axis, dim in sides:
        count = lax.axis_size(axis)
        ends = count - 1
        head = lax.slice_in_dim(cells, 0, width, axis=dim)
        tail = lax.slice_in_dim(cells, cells.shape[dim] - width, cells.shape[dim], axis=dim)
        cells = jnp.concatenate(
            [
                lax.ppermute(tail, axis, [(i, (i + 1) % count) for i in range(ends)]),
                cells,
                lax.ppermute(head, axis, [((i + 1) % count, i) for i in range(ends)]),
            ],
            axis=dim,
        )
    return cells


def row_pass(extended, half_widths):
    total_rows = extended.shape[1]
    out_rows = total_rows - 2 * HW_MAX
    out_index = lax.broadcasted_iota(jnp.int32, (out_rows, total_rows), 0)
    in_index = lax.broadcasted_iota(jnp.int32, (out_rows, total_rows), 1)
    distance = jnp.abs(in_index - HW_MAX - out_index)
    row_band = (distance[None] <= half_widths[:, None, None]).astype(jnp.float32)
    return jnp.einsum(
        "kim,kmj->kij",
        row_band,
        extended,
        precision=lax.Precision.HIGHEST,
        preferred_element_type=jnp.float32,
    )


def column_pass(extended, half_widths):
    total_cols = extended.shape[2]
    out_cols = total_cols - 2 * HW_MAX
    in_index = lax.broadcasted_iota(jnp.int32, (total_cols, out_cols), 0)
    out_index = lax.broadcasted_iota(jnp.int32, (total_cols, out_cols), 1)
    distance = jnp.abs(in_index - HW_MAX - out_index)
    col_band = (distance[None] <= half_widths[:, None, None]).astype(jnp.float32)
    return jnp.einsum(
        "kim,kmj->kij",
        extended,
        col_band,
        precision=lax.Precision.HIGHEST,
        preferred_element_type=jnp.float32,
    )


def body(beam_images, chan_weights, freq_offsets, half_widths):
    local_chans = beam_images.shape[0]
    slab_rows = beam_images.shape[1]
    all_cols = beam_images.shape[2]
    weight_floats = chan_weights.astype(jnp.float32)
    weight_total = lax.psum(jnp.sum(weight_floats), "chan")
    powers = jnp.stack([freq_offsets**power for power in range(MOMENTS)])
    coefficients = powers * weight_floats[None, :] / weight_total
    flat = beam_images.reshape(local_chans, slab_rows * all_cols)
    partials = jnp.dot(
        coefficients, flat, precision=lax.Precision.HIGHEST, preferred_element_type=jnp.float32
    )
    partials = partials.reshape(MOMENTS, slab_rows, all_cols)
    shares = lax.psum_scatter(partials, "chan", scatter_dimension=2, tiled=True)
    extended = padded(shares, (("chan", 2), ("slab", 1)), HW_MAX)
    summed = column_pass(row_pass(extended, half_widths), half_widths)
    divisor = (2 * half_widths + 1).astype(jnp.float32)
    return summed / divisor[:, None, None]


def solution(mesh):
    placed = (P("chan", "slab", None), P("chan"), P("chan"), P())
    return jax.shard_map(
        body, mesh=mesh, in_specs=placed, out_specs=P(None, "slab", "chan"), check_vma=False
    )
```

profile of v0, /device:TPU:9, one launch (start us, length us, event | category | flops | bytes accessed | tf_op | source)
XLA Modules:
  0.0 180.7 jit_solution(14142702040330019282)
XLA Ops:
  6.5 0.0 reduce-scatter.2.cloned.1.call-start
  6.5 0.7 multiply_bitcast_fusion
  7.2 1.3 convert_reduce_fusion
  8.5 0.7 convert_element_type.8
  9.1 6.3 %psum.7 = f32[]{:T(128)} all-reduce(f32[]{:T(128)} %convert_reduce_fusion), channel_id=1, replica_groups=mesh['chan'=4,'slab'=8] {'chan'}, use_global_device_ids=true, to_apply=%region_1.0 | all-reduce | flops 1 | bytes 8 | tf_op jit(solution)/shard_map/psum | solution.py:64
  15.4 0.7 stack.19
  16.1 25.8 %fusion.2 = f32[5,64,4096]{2,0,1:T(8,128)} fusion(f32[5,16]{1,0:T(8,128)S(1)} %stack.19, f32[]{:T(128)} %psum.7, f32[16]{0:T(128)S(1)} %convert_element_type.8, f32[2,8,64,4096]{3,2,1,0:T(8,128)} %bitcast.22), kind=kOutput, calls=%fused_computation.2 | convolution fusion | flops 251658400 | bytes 22020484 | tf_op jit(solution)/shard_map/dot_general | solution.py:68
  41.9 0.0 copy-start
  41.9 0.0 reduce-scatter.2.cloned.1.call-update
  42.0 72.7 %reduce-scatter.2.cloned.1.call-done = f32[5,64,1024]{2,0,1:T(8,128)} async-done(((f32[5,64,4096]{2,0,1:T(8,128)}), f32[5,64,1024]{2,0,1:T(8,128)}) %reduce-scatter.2.cloned.1.call-update) | async-done | bytes 1310736 | tf_op jit(solution)/shard_map/reduce_scatter | solution.py:72
  114.6 1.2 fusion.21
  115.8 2.9 %collective-permute-start = (f32[5,64,32]{2,0,1:T(8,128)S(1)}, f32[5,64,32]{2,0,1:T(8,128)S(1)}, u32[]{:S(2)}, u32[]{:S(2)}) collective-permute-start(f32[5,64,32]{2,0,1:T(8,128)S(1)} %get-tuple-element.8), channel_id=1, source_target_pairs={{0,8},{8,16},{16,24},{1,9},{9,17},{17,25},{2,10},{10,18},{18,26},{... | collective-permute-start | bytes 122888 | tf_op jit(solution)/shard_map/ppermute | solution.py:18
  118.7 1.9 %collective-permute-start.1 = (f32[5,64,32]{2,0,1:T(8,128)S(1)}, f32[5,64,32]{2,0,1:T(8,128)S(1)}, u32[]{:S(2)}, u32[]{:S(2)}) collective-permute-start(f32[5,64,32]{2,0,1:T(8,128)S(1)} %get-tuple-element.7), channel_id=1, source_target_pairs={{8,0},{16,8},{24,16},{9,1},{17,9},{25,17},{10,2},{18,10},{26,18},{... | collective-permute-start | bytes 122888 | tf_op jit(solution)/shard_map/ppermute | solution.py:20
  120.6 0.0 copy-done
  120.7 1.3 collective-permute-done
  122.0 4.4 %collective-permute-done.1 = f32[5,64,32]{2,0,1:T(8,128)S(1)} collective-permute-done((f32[5,64,32]{2,0,1:T(8,128)S(1)}, f32[5,64,32]{2,0,1:T(8,128)S(1)}, u32[]{:S(2)}, u32[]{:S(2)}) %collective-permute-start.1) | collective-permute-done | bytes 40992 | tf_op jit(solution)/shard_map/ppermute | solution.py:20
  126.4 3.1 %concatenate.6 = f32[5,64,1088]{2,0,1:T(8,128)S(1)} concatenate(f32[5,64,32]{2,0,1:T(8,128)S(1)} %collective-permute-done, f32[5,64,1024]{2,0,1:T(8,128)} %reduce-scatter.2.cloned.1.call-done, f32[5,64,32]{2,0,1:T(8,128)S(1)} %collective-permute-done.1), dimensions={2} | concatenate | bytes 2785280 | tf_op jit(solution)/shard_map/concatenate | solution.py:16
  129.5 0.2 fusion.20
  129.6 0.1 copy.8
  129.8 3.1 %collective-permute-start.3 = (f32[5,32,1088]{2,1,0:T(8,128)S(1)}, f32[5,32,1088]{2,1,0:T(8,128)S(1)}, u32[]{:S(2)}, u32[]{:S(2)}) collective-permute-start(f32[5,32,1088]{2,1,0:T(8,128)S(1)} %copy.8), channel_id=1, source_target_pairs={{1,0},{2,1},{3,2},{4,3},{5,4},{6,5},{7,6},{9,8},{10,9},{11,10},{12... | collective-permute-start | bytes 2088968 | tf_op jit(solution)/shard_map/ppermute | solution.py:20
  132.9 0.1 copy.7
  133.0 2.4 %collective-permute-start.2 = (f32[5,32,1088]{2,1,0:T(8,128)S(1)}, f32[5,32,1088]{2,1,0:T(8,128)S(1)}, u32[]{:S(2)}, u32[]{:S(2)}) collective-permute-start(f32[5,32,1088]{2,1,0:T(8,128)S(1)} %copy.7), channel_id=1, source_target_pairs={{0,1},{1,2},{2,3},{3,4},{4,5},{5,6},{6,7},{8,9},{9,10},{10,11},{11... | collective-permute-start | bytes 2088968 | tf_op jit(solution)/shard_map/ppermute | solution.py:18
  135.4 0.6 subtract_abs_fusion
  136.1 25.8 %collective-permute-done.3 = f32[5,32,1088]{2,1,0:T(8,128)S(1)} collective-permute-done((f32[5,32,1088]{2,1,0:T(8,128)S(1)}, f32[5,32,1088]{2,1,0:T(8,128)S(1)}, u32[]{:S(2)}, u32[]{:S(2)}) %collective-permute-start.3) | collective-permute-done | bytes 696352 | tf_op jit(solution)/shard_map/ppermute | solution.py:20
  161.9 0.5 copy.10
  162.4 0.0 collective-permute-done.2
  162.4 0.5 copy.9
  162.8 0.5 pad_maximum_fusion
  163.3 1.5 fusion.7
  164.9 9.0 %fusion.9 = f32[5,64,1024]{2,1,0:T(8,128)} fusion(f32[5,64,1088]{2,1,0:T(8,128)S(1)} %fusion.7, s32[1088,1024]{1,0:T(8,128)S(1)} %subtract_abs_fusion, s32[5]{0:T(128)S(1)} %copy-done, f32[5]{0:T(128)S(1)} %add_convert_fusion), kind=kOutput, calls=%fused_computation.11 | convolution fusion | flops 4284088320 | bytes 7159848 | tf_op jit(solution)/shard_map/kim,kmj->kij/dot_general | solution.py:50
  (5 shorter events, 0.0 us)
Async XLA Ops:
  6.5 108.1 %reduce-scatter.2.cloned.1.call-start = ((), (), s32[]{:S(2)}) async-start(), calls=%async_computation.1 | async-start | bytes 10485760 | tf_op jit(solution)/shard_map/reduce_scatter | solution.py:72
  41.9 78.7 %copy-start = (s32[5]{0:T(128)S(1)}, s32[5]{0:T(128)}, u32[]{:S(2)}) copy-start(s32[5]{0:T(128)} %param.7) | copy-start | bytes 64
  115.8 6.2 %collective-permute-start = (f32[5,64,32]{2,0,1:T(8,128)S(1)}, f32[5,64,32]{2,0,1:T(8,128)S(1)}, u32[]{:S(2)}, u32[]{:S(2)}) collective-permute-start(f32[5,64,32]{2,0,1:T(8,128)S(1)} %get-tuple-element.8), channel_id=1, source_target_pairs={{0,8},{8,16},{16,24},{1,9},{9,17},{17,25},{2,10},{10,18},{18,26},{... | collective-permute-start | bytes 122888 | tf_op jit(solution)/shard_map/ppermute | solution.py:18
  118.7 7.7 %collective-permute-start.1 = (f32[5,64,32]{2,0,1:T(8,128)S(1)}, f32[5,64,32]{2,0,1:T(8,128)S(1)}, u32[]{:S(2)}, u32[]{:S(2)}) collective-permute-start(f32[5,64,32]{2,0,1:T(8,128)S(1)} %get-tuple-element.7), channel_id=1, source_target_pairs={{8,0},{16,8},{24,16},{9,1},{17,9},{25,17},{10,2},{18,10},{26,18},{... | collective-permute-start | bytes 122888 | tf_op jit(solution)/shard_map/ppermute | solution.py:20
  129.8 32.1 %collective-permute-start.3 = (f32[5,32,1088]{2,1,0:T(8,128)S(1)}, f32[5,32,1088]{2,1,0:T(8,128)S(1)}, u32[]{:S(2)}, u32[]{:S(2)}) collective-permute-start(f32[5,32,1088]{2,1,0:T(8,128)S(1)} %copy.8), channel_id=1, source_target_pairs={{1,0},{2,1},{3,2},{4,3},{5,4},{6,5},{7,6},{9,8},{10,9},{11,10},{12... | collective-permute-start | bytes 2088968 | tf_op jit(solution)/shard_map/ppermute | solution.py:20
  133.0 29.4 %collective-permute-start.2 = (f32[5,32,1088]{2,1,0:T(8,128)S(1)}, f32[5,32,1088]{2,1,0:T(8,128)S(1)}, u32[]{:S(2)}, u32[]{:S(2)}) collective-permute-start(f32[5,32,1088]{2,1,0:T(8,128)S(1)} %copy.7), channel_id=1, source_target_pairs={{0,1},{1,2},{2,3},{3,4},{4,5},{5,6},{6,7},{8,9},{9,10},{10,11},{11... | collective-permute-start | bytes 2088968 | tf_op jit(solution)/shard_map/ppermute | solution.py:18
Sparse Core Ops, SparseCore 0:
  42.0 72.5 reduce-scatter.1
where the time goes:
time: 182 us; the launch traced here: 181 us
  waiting for transfers between devices  104 us (57%)
  matrix products  36.4 us (20%)
  between operations  13.5 us (7%)
  starting transfers between devices  10.3 us (6%)
  blocking collectives  6.29 us (3%)
  local copies, waits for them, and re-layouts  6.27 us (3%)
  other arithmetic  3.71 us (2%)
    reduce_scatter x1, waiting for transfers between devices, body(): shares = lax.psum_scatter(partials, 'chan', scatter_dimension=2, tiled=True)  72.7 us
    ppermute x2, waiting for transfers between devices, padded(): lax.ppermute(head, axis, [((i + 1) % count, i) for i in range(ends)])  30.2 us
    dot_general x1, matrix products, body(): jnp.dot(coefficients, flat, precision=lax.Precision.HIGHEST, preferred_el...  25.8 us
    dot_general x1, matrix products, column_pass(): jnp.einsum('kim,kmj->kij', extended, col_band, precision=lax.Precision.HI...  9.02 us
    psum x1, blocking collectives, body(): weight_total = lax.psum(jnp.sum(weight_floats), 'chan')  6.29 us
    ppermute x2, starting transfers between devices, padded(): lax.ppermute(tail, axis, [(i, (i + 1) % count) for i in range(ends)])  5.31 us
    ppermute x2, starting transfers between devices, padded(): lax.ppermute(head, axis, [((i + 1) % count, i) for i in range(ends)])  4.98 us
  transfers between devices with their start and end apart: 5, of which 4 were waited for; matrix products, arithmetic and copies ran while one was open for 1% of the time, Pallas kernels for 0%

commit v1 on v0

v1 whole, which is shorter than its diff:
```python
import functools

import jax
import jax.numpy as jnp
from jax import lax
from jax.experimental import pallas as pl
from jax.experimental.pallas import tpu as pltpu
from jax.sharding import PartitionSpec as P

MOMENTS = 5
HW_MAX = 32
LANES = 128
STEP = 2 * LANES
PARTS = 2
ROWS_AT_ONCE = 32
MESH = pl.DeviceIdType.MESH


def split(value):
    parts = []
    for _ in range(PARTS - 1):
        part = value.astype(jnp.bfloat16)
        parts.append(part)
        value = value - part.astype(jnp.float32)
    parts.append(value.astype(jnp.bfloat16))
    return parts


def kernel(
    chans, slabs,
    w_ref, f_ref, h_ref, beam_ref, out_ref,
    beams, pieces, band, row_band, sums, passed, crossed, ext, done, weights,
    load_sem, pass_send, pass_recv, cross_send, cross_recv,
    up_send, up_recv, down_send, down_recv, out_sem, w_send, w_recv,
):
    groups = chans // 2
    me = lax.axis_index("chan")
    slab = lax.axis_index("slab")
    group, core = me // 2, lax.rem(me, 2)
    local_chans, rows, all_cols = beam_ref.shape
    width = all_cols // chans
    steps = width // STEP
    tiles = width // LANES + 2
    chunks = width // LANES
    partner = group * 2 + (1 - core)
    not_first, not_last = slab > 0, slab < slabs - 1

    def block_of(slot):
        owner_group = lax.rem(group + slot // 2 + 1, groups)
        return owner_group * 2 + (1 - core if slot % 2 == 0 else core)

    def tile_col(slot, tile):
        return block_of(slot) * width + (tile - 1) * LANES

    def load(slot, tile):
        col = pl.multiple_of(tile_col(slot, tile), LANES)
        return pltpu.make_async_copy(
            beam_ref.at[:, :, pl.ds(col, LANES)], beams.at[slot, tile], load_sem.at[slot, tile]
        )

    def inside(slot, tile):
        col = tile_col(slot, tile)
        return jnp.logical_and(col >= 0, col < all_cols)

    def start_load(slot, tile):
        @pl.when(inside(slot, tile))
        def _():
            load(slot, tile).start()

    for slot in range(chans):
        @pl.loop(0, 4)
        def _(tile):
            start_load(slot, tile)

    @pl.loop(4, tiles)
    def _(tile):
        for slot in range(chans):
            start_load(slot, tile)

    barrier = pltpu.get_barrier_semaphore()
    for offset in range(1, chans):
        pl.semaphore_signal(
            barrier, inc=1, device_id={"chan": lax.rem(me + offset, chans)}, device_id_type=MESH
        )

    @pl.when(not_first)
    def _():
        pl.semaphore_signal(barrier, inc=1, device_id={"slab": slab - 1}, device_id_type=MESH)

    @pl.when(not_last)
    def _():
        pl.semaphore_signal(barrier, inc=1, device_id={"slab": slab + 1}, device_id_type=MESH)

    total = w_ref[0].astype(jnp.float32)
    for chan in range(1, local_chans):
        total = total + w_ref[chan].astype(jnp.float32)
    weights[0] = jnp.full(weights.shape[1:], total, jnp.float32)

    @pl.loop(0, MOMENTS)
    def _(k):
        reach = h_ref[k]
        for at in range(0, 2 * STEP, LANES):
            source = lax.broadcasted_iota(jnp.int32, (LANES, STEP), 0) + at
            target = lax.broadcasted_iota(jnp.int32, (LANES, STEP), 1)
            near = jnp.abs(source - LANES - target) <= reach
            band[k, at : at + LANES, :] = jnp.where(near, 1.0, 0.0).astype(jnp.bfloat16)
        span = rows + 2 * HW_MAX
        target = lax.broadcasted_iota(jnp.int32, (rows, span), 0)
        source = lax.broadcasted_iota(jnp.int32, (rows, span), 1)
        near = jnp.abs(source - HW_MAX - target) <= reach
        near = jnp.where(near, 1.0, 0.0).astype(jnp.bfloat16)
        for part in range(PARTS):
            row_band[k, :, part * span : (part + 1) * span] = near

    @pl.when(slab == 0)
    def _():
        @pl.loop(0, chunks)
        def _(i):
            ext[i, :, 0:HW_MAX, :] = jnp.zeros((MOMENTS, HW_MAX, LANES), jnp.float32)

    @pl.when(slab == slabs - 1)
    def _():
        @pl.loop(0, chunks)
        def _(i):
            ext[i, :, HW_MAX + rows :, :] = jnp.zeros((MOMENTS, HW_MAX, LANES), jnp.float32)

    pl.semaphore_wait(
        barrier, chans - 1 + not_first.astype(jnp.int32) + not_last.astype(jnp.int32)
    )

    def weight_copy(offset):
        return pltpu.make_async_remote_copy(
            src_ref=weights.at[0], dst_ref=weights.at[offset],
            send_sem=w_send.at[offset - 1], recv_sem=w_recv.at[offset - 1],
            device_id={"chan": lax.rem(me + offset, chans)}, device_id_type=MESH,
        )

    def pass_copy(hop, j):
        return pltpu.make_async_remote_copy(
            src_ref=sums.at[2 * hop, pl.ds(2 * j, 2)], dst_ref=passed.at[hop, pl.ds(2 * j, 2)],
            send_sem=pass_send.at[hop, j], recv_sem=pass_recv.at[hop, j],
            device_id={"chan": partner}, device_id_type=MESH,
        )

    def cross_copy(hop, i):
        other = lax.rem(group + hop + 1, groups) * 2 + core
        return pltpu.make_async_remote_copy(
            src_ref=sums.at[2 * hop + 1, i], dst_ref=crossed.at[hop, i],
            send_sem=cross_send.at[hop, i], recv_sem=cross_recv.at[hop, i],
            device_id={"chan": other}, device_id_type=MESH,
        )

    def up_copy(i):
        return pltpu.make_async_remote_copy(
            src_ref=ext.at[i, :, pl.ds(HW_MAX, HW_MAX)],
            dst_ref=ext.at[i, :, pl.ds(HW_MAX + rows, HW_MAX)],
            send_sem=up_send.at[i], recv_sem=up_recv.at[i],
            device_id={"slab": slab - 1}, device_id_type=MESH,
        )

    def down_copy(i):
        return pltpu.make_async_remote_copy(
            src_ref=ext.at[i, :, pl.ds(rows, HW_MAX)],
            dst_ref=ext.at[i, :, pl.ds(0, HW_MAX)],
            send_sem=down_send.at[i], recv_sem=down_recv.at[i],
            device_id={"slab": slab + 1}, device_id_type=MESH,
        )

    def out_copy(i):
        return pltpu.make_async_copy(
            done.at[i], out_ref.at[:, :, pl.ds(pl.multiple_of(i * LANES, LANES), LANES)],
            out_sem.at[i],
        )

    for offset in range(1, chans):
        weight_copy(offset).start()

    def moments_of(slot, tile):
        valid = inside(slot, tile)

        @pl.when(valid)
        def _():
            load(slot, tile).wait()

        @pl.when(jnp.logical_not(valid))
        def _():
            beams[slot, tile] = jnp.zeros(beams.shape[2:], jnp.float32)

        cols = pl.ds(pl.multiple_of(tile * LANES, LANES), LANES)

        @pl.loop(0, rows // ROWS_AT_ONCE)
        def _(part):
            first = pl.multiple_of(part * ROWS_AT_ONCE, ROWS_AT_ONCE)
            totals = [None] * MOMENTS
            for chan in range(local_chans):
                weight = w_ref[chan].astype(jnp.float32)
                offset = f_ref[chan]
                term = beams[slot, tile, chan, pl.ds(first, ROWS_AT_ONCE), :] * weight
                for k in range(MOMENTS):
                    if k > 0:
                        term = term * offset
                    totals[k] = term if chan == 0 else totals[k] + term
            for k in range(MOMENTS):
                for at, piece in enumerate(split(totals[k])):
                    pieces[slot, k, pl.ds(first + at * rows, ROWS_AT_ONCE), cols] = piece

    def columns_of(slot, j):
        wide = pl.ds(pl.multiple_of(j * STEP, STEP), 2 * STEP)

        @pl.loop(0, MOMENTS)
        def _(k):
            product = jnp.dot(
                pieces[slot, k, :, wide], band[k], preferred_element_type=jnp.float32
            )
            result = product[:rows]
            for at in range(1, PARTS):
                result = result + product[at * rows : (at + 1) * rows]
            sums[slot, 2 * j, k] = result[:, :LANES]
            sums[slot, 2 * j + 1, k] = result[:, LANES:]

    def step(j, first_tile, last_tile):
        def make(slot):
            @pl.loop(first_tile, last_tile)
            def _(tile):
                moments_of(slot, tile)

            columns_of(slot, j)

        for hop in range(groups):
            make(2 * hop)
            pass_copy(hop, j).start()
            make(2 * hop + 1)
            pass_copy(hop, j).wait_recv()
            for half in range(2):
                i = 2 * j + half
                sums[2 * hop + 1, i] = sums[2 * hop + 1, i] + passed[hop, i]
                if hop < groups - 1:
                    cross_copy(hop, i).start()

    def finish(i):
        value = sums[chans - 1, i]
        for hop in range(groups - 1):
            cross_copy(hop, i).wait_recv()
            value = value + crossed[hop, i]
        ext[i, :, HW_MAX : HW_MAX + rows, :] = value

        @pl.when(not_first)
        def _():
            up_copy(i).start()

        @pl.when(not_last)
        def _():
            down_copy(i).start()

    def rows_of(i):
        @pl.when(not_last)
        def _():
            up_copy(i).wait_recv()

        @pl.when(not_first)
        def _():
            down_copy(i).wait_recv()

        weight_total = weights[0]
        for offset in range(1, chans):
            weight_total = weight_total + weights[offset]
        for k in range(MOMENTS):
            both = jnp.concatenate(split(ext[i, k]), axis=0)
            summed = jnp.dot(row_band[k], both, preferred_element_type=jnp.float32)
            divisor = weight_total * (2 * h_ref[k] + 1).astype(jnp.float32)
            done[i, k] = summed * (1.0 / divisor)[0:1, :]
        out_copy(i).start()

    step(0, 0, 4)

    @pl.loop(1, steps - 1)
    def _(j):
        step(j, 2 * j + 2, 2 * j + 4)

    finish(0)
    step(steps - 1, 2 * steps, 2 * steps + 2)
    finish(1)
    for offset in range(1, chans):
        weight_copy(offset).wait_recv()

    @pl.loop(2, chunks)
    def _(i):
        finish(i)
        rows_of(i - 2)

    @pl.loop(chunks - 2, chunks)
    def _(i):
        rows_of(i)

    for offset in range(1, chans):
        weight_copy(offset).wait_send()

    @pl.loop(0, steps)
    def _(j):
        for hop in range(groups):
            pass_copy(hop, j).wait_send()

    @pl.loop(0, chunks)
    def _(i):
        for hop in range(groups - 1):
            cross_copy(hop, i).wait_send()

        @pl.when(not_first)
        def _():
            up_copy(i).wait_send()

        @pl.when(not_last)
        def _():
            down_copy(i).wait_send()

        out_copy(i).wait()


def body(chans, slabs, beam_images, chan_weights, freq_offsets, half_widths):
    local_chans, rows, all_cols = beam_images.shape
    width = all_cols // chans
    chunks, steps, tiles, groups = width // LANES, width // STEP, width // LANES + 2, chans // 2
    f32, b16 = jnp.float32, jnp.bfloat16
    dma = pltpu.SemaphoreType.DMA
    smem = pl.BlockSpec(memory_space=pltpu.SMEM)
    anywhere = pl.BlockSpec(memory_space=pl.ANY)
    span = rows + 2 * HW_MAX
    return pl.pallas_call(
        functools.partial(kernel, chans, slabs),
        out_shape=jax.ShapeDtypeStruct((MOMENTS, rows, width), f32),
        in_specs=[smem, smem, smem, anywhere],
        out_specs=anywhere,
        scratch_shapes=[
            pltpu.VMEM((chans, tiles, local_chans, rows, LANES), f32),
            pltpu.VMEM((chans, MOMENTS, PARTS * rows, tiles * LANES), b16),
            pltpu.VMEM((MOMENTS, 2 * STEP, STEP), b16),
            pltpu.VMEM((MOMENTS, rows, PARTS * span), b16),
            pltpu.VMEM((chans, chunks, MOMENTS, rows, LANES), f32),
            pltpu.VMEM((groups, chunks, MOMENTS, rows, LANES), f32),
            pltpu.VMEM((groups - 1, chunks, MOMENTS, rows, LANES), f32),
            pltpu.VMEM((chunks, MOMENTS, span, LANES), f32),
            pltpu.VMEM((chunks, MOMENTS, rows, LANES), f32),
            pltpu.VMEM((chans, 8, LANES), f32),
            dma((chans, tiles)),
            dma((groups, steps)),
            dma((groups, steps)),
            dma((groups - 1, chunks)),
            dma((groups - 1, chunks)),
            dma((chunks,)),
            dma((chunks,)),
            dma((chunks,)),
            dma((chunks,)),
            dma((chunks,)),
            dma((chans - 1,)),
            dma((chans - 1,)),
        ],
        compiler_params=pltpu.CompilerParams(
            collective_id=0, has_side_effects=True, vmem_limit_bytes=60 * 1024 * 1024
        ),
    )(chan_weights, freq_offsets, half_widths, beam_images)


def solution(mesh):
    placed = (P("chan", "slab", None), P("chan"), P("chan"), P())
    return jax.shard_map(
        functools.partial(body, mesh.shape["chan"], mesh.shape["slab"]),
        mesh=mesh, in_specs=placed, out_specs=P(None, "slab", "chan"), check_vma=False,
    )
```

time: 182 us -> 59.4 us (0.33)
  waiting for transfers between devices: 104 us -> 0 us
  Pallas kernels: 0 us -> 56.7 us
  matrix products: 36.4 us -> 0 us
  between operations: 13.5 us -> 0.01 us
  starting transfers between devices: 10.3 us -> 0 us
  blocking collectives: 6.29 us -> 0 us
  local copies, waits for them, and re-layouts: 6.27 us -> 2.52 us
  other arithmetic: 3.71 us -> 0 us
    reduce_scatter x1 -> x0, waiting for transfers between devices: 72.7 us -> none  [body(): shares = lax.psum_scatter(partials, 'chan', scatter_dimension=2, tiled=True)]
    pallas_call x0 -> x1, Pallas kernels: none -> 56.7 us  [body(): pl.pallas_call(functools.partial(kernel, chans, slabs), out_shape=jax.Sha...]
    dot_general x3 -> x0, matrix products: 36.4 us -> none  [the longest x1 25.8 us: body(): jnp.dot(coefficients, flat, precision=lax.Precision.HIGHEST, preferred_el...]
    ppermute x4 -> x0, waiting for transfers between devices: 31.6 us -> none  [the longest x2 30.2 us: padded(): lax.ppermute(head, axis, [((i + 1) % count, i) for i in range(ends)])]
    ppermute x4 -> x0, starting transfers between devices: 10.3 us -> none  [the longest x2 5.31 us: padded(): lax.ppermute(tail, axis, [(i, (i + 1) % count) for i in range(ends)])]
    psum x1 -> x0, blocking collectives: 6.29 us -> none  [body(): weight_total = lax.psum(jnp.sum(weight_floats), 'chan')]
    concatenate x1 -> x0, local copies, waits for them, and re-layouts: 3.07 us -> none  [padded(): jnp.concatenate([lax.ppermute(tail, axis, [(i, (i + 1) % count) for i in...]
    unnamed x2 -> x1, local copies, waits for them, and re-layouts: 0.01 us -> 2.52 us
  transfers between devices with their start and end apart: 5 -> 0, of which waited for: 4 -> 0; matrix products, arithmetic and copies ran while one was open for 1% -> 0% of each run, Pallas kernels for 0% -> 0%
where the time goes in v1:
time: 59.4 us; the launch traced here: 59.2 us
  Pallas kernels  56.7 us (95%)
  local copies, waits for them, and re-layouts  2.52 us (4%)
    pallas_call x1, Pallas kernels, body(): pl.pallas_call(functools.partial(kernel, chans, slabs), out_shape=jax.Sha...  56.7 us
    unnamed x1, local copies, waits for them, and re-layouts  2.52 us

profile of v1, /device:TPU:9, one launch (start us, length us, event | category | flops | bytes accessed | tf_op | source)
XLA Modules:
  0.0 59.2 jit_solution(557665168382123068)
XLA Ops:
  0.0 56.7 %shard_map.46 = f32[5,64,1024]{2,1,0:T(8,128)} custom-call(s32[16]{0:T(128)} %w_ref.1, f32[16]{0:T(128)} %f_ref.1, s32[5]{0:T(128)} %h_ref.1, f32[16,64,4096]{2,1,0:T(8,128)} %beam_ref.1), custom_call_target="tpu_custom_call" | custom-call | tf_op jit(solution)/shard_map/pallas_call | solution.py:328
  56.7 2.5 %copy.6 = f32[5,64,1024]{2,1,0:T(8,128)} copy(f32[5,64,1024]{2,1,0:T(8,128)} %shard_map.46) | data formatting | bytes 2621440

commit v2 on v1

--- a/solution.py
+++ b/solution.py
@@ -207,8 +207,7 @@
     def columns_of(slot, j):
         wide = pl.ds(pl.multiple_of(j * STEP, STEP), 2 * STEP)
 
-        @pl.loop(0, MOMENTS)
-        def _(k):
+        for k in range(MOMENTS):
             product = jnp.dot(
                 pieces[slot, k, :, wide], band[k], preferred_element_type=jnp.float32
             )
@@ -272,20 +271,24 @@
         out_copy(i).start()
 
     step(0, 0, 4)
-
-    @pl.loop(1, steps - 1)
+    for offset in range(1, chans):
+        weight_copy(offset).wait_recv()
+
+    @pl.loop(1, steps)
     def _(j):
         step(j, 2 * j + 2, 2 * j + 4)
-
-    finish(0)
-    step(steps - 1, 2 * steps, 2 * steps + 2)
-    finish(1)
-    for offset in range(1, chans):
-        weight_copy(offset).wait_recv()
-
-    @pl.loop(2, chunks)
+        finish(j - 1)
+
+    @pl.loop(steps - 1, chunks)
     def _(i):
         finish(i)
+
+        @pl.when(i == steps - 1)
+        def _():
+            @pl.loop(0, steps - 3)
+            def _(late):
+                rows_of(late)
+
         rows_of(i - 2)
 
     @pl.loop(chunks - 2, chunks)

time: 59.4 us -> 50 us (0.84)
  Pallas kernels: 56.7 us -> 47.3 us
    pallas_call x1, Pallas kernels: 56.7 us -> 47.3 us  [body(): pl.pallas_call(functools.partial(kernel, chans, slabs), out_shape=jax.Sha...]
where the time goes in v2:
time: 50 us; the launch traced here: 49.8 us
  Pallas kernels  47.3 us (95%)
  local copies, waits for them, and re-layouts  2.52 us (5%)
    pallas_call x1, Pallas kernels, body(): pl.pallas_call(functools.partial(kernel, chans, slabs), out_shape=jax.Sha...  47.3 us
    unnamed x1, local copies, waits for them, and re-layouts  2.52 us

profile of v2, /device:TPU:9, one launch (start us, length us, event | category | flops | bytes accessed | tf_op | source)
XLA Modules:
  0.0 49.8 jit_solution(6998383633579288945)
XLA Ops:
  0.0 47.3 %shard_map.46 = f32[5,64,1024]{2,1,0:T(8,128)} custom-call(s32[16]{0:T(128)} %w_ref.1, f32[16]{0:T(128)} %f_ref.1, s32[5]{0:T(128)} %h_ref.1, f32[16,64,4096]{2,1,0:T(8,128)} %beam_ref.1), custom_call_target="tpu_custom_call" | custom-call | tf_op jit(solution)/shard_map/pallas_call | solution.py:331
  47.3 2.5 %copy.6 = f32[5,64,1024]{2,1,0:T(8,128)} copy(f32[5,64,1024]{2,1,0:T(8,128)} %shard_map.46) | data formatting | bytes 2621440

commit v3 on v2

--- a/solution.py
+++ b/solution.py
@@ -29,9 +29,9 @@
 def kernel(
     chans, slabs,
     w_ref, f_ref, h_ref, beam_ref, out_ref,
-    beams, pieces, band, row_band, sums, passed, crossed, ext, done, weights,
+    beams, pieces, band, row_band, sums, passed, crossed, ext, weights,
     load_sem, pass_send, pass_recv, cross_send, cross_recv,
-    up_send, up_recv, down_send, down_recv, out_sem, w_send, w_recv,
+    up_send, up_recv, down_send, down_recv, w_send, w_recv,
 ):
     groups = chans // 2
     me = lax.axis_index("chan")
@@ -166,12 +166,6 @@
             device_id={"slab": slab + 1}, device_id_type=MESH,
         )
 
-    def out_copy(i):
-        return pltpu.make_async_copy(
-            done.at[i], out_ref.at[:, :, pl.ds(pl.multiple_of(i * LANES, LANES), LANES)],
-            out_sem.at[i],
-        )
-
     for offset in range(1, chans):
         weight_copy(offset).start()
 
@@ -217,7 +211,7 @@
             sums[slot, 2 * j, k] = result[:, :LANES]
             sums[slot, 2 * j + 1, k] = result[:, LANES:]
 
-    def step(j, first_tile, last_tile):
+    def step(j, first_tile, last_tile, hops):
         def make(slot):
             @pl.loop(first_tile, last_tile)
             def _(tile):
@@ -225,7 +219,7 @@
 
             columns_of(slot, j)
 
-        for hop in range(groups):
+        for hop in hops:
             make(2 * hop)
             pass_copy(hop, j).start()
             make(2 * hop + 1)
@@ -267,17 +261,20 @@
             both = jnp.concatenate(split(ext[i, k]), axis=0)
             summed = jnp.dot(row_band[k], both, preferred_element_type=jnp.float32)
             divisor = weight_total * (2 * h_ref[k] + 1).astype(jnp.float32)
-            done[i, k] = summed * (1.0 / divisor)[0:1, :]
-        out_copy(i).start()
-
-    step(0, 0, 4)
+            out_ref[k, :, pl.ds(pl.multiple_of(i * LANES, LANES), LANES)] = (
+                summed * (1.0 / divisor)[0:1, :]
+            )
+
+    step(0, 0, 4, range(groups))
+
+    @pl.loop(1, steps)
+    def _(j):
+        step(j, 2 * j + 2, 2 * j + 4, range(groups - 1))
+        finish(j - 1)
+        step(j, 2 * j + 2, 2 * j + 4, range(groups - 1, groups))
+
     for offset in range(1, chans):
         weight_copy(offset).wait_recv()
-
-    @pl.loop(1, steps)
-    def _(j):
-        step(j, 2 * j + 2, 2 * j + 4)
-        finish(j - 1)
 
     @pl.loop(steps - 1, chunks)
     def _(i):
@@ -315,8 +312,6 @@
         @pl.when(not_last)
         def _():
             down_copy(i).wait_send()
-
-        out_copy(i).wait()
 
 
 def body(chans, slabs, beam_images, chan_weights, freq_offsets, half_widths):
@@ -332,7 +327,7 @@
         functools.partial(kernel, chans, slabs),
         out_shape=jax.ShapeDtypeStruct((MOMENTS, rows, width), f32),
         in_specs=[smem, smem, smem, anywhere],
-        out_specs=anywhere,
+        out_specs=pl.BlockSpec(memory_space=pltpu.VMEM),
         scratch_shapes=[
             pltpu.VMEM((chans, tiles, local_chans, rows, LANES), f32),
             pltpu.VMEM((chans, MOMENTS, PARTS * rows, tiles * LANES), b16),
@@ -342,7 +337,6 @@
             pltpu.VMEM((groups, chunks, MOMENTS, rows, LANES), f32),
             pltpu.VMEM((groups - 1, chunks, MOMENTS, rows, LANES), f32),
             pltpu.VMEM((chunks, MOMENTS, span, LANES), f32),
-            pltpu.VMEM((chunks, MOMENTS, rows, LANES), f32),
             pltpu.VMEM((chans, 8, LANES), f32),
             dma((chans, tiles)),
             dma((groups, steps)),
@@ -353,12 +347,11 @@
             dma((chunks,)),
             dma((chunks,)),
             dma((chunks,)),
-            dma((chunks,)),
             dma((chans - 1,)),
             dma((chans - 1,)),
         ],
         compiler_params=pltpu.CompilerParams(
-            collective_id=0, has_side_effects=True, vmem_limit_bytes=60 * 1024 * 1024
+            collective_id=0, has_side_effects=True, vmem_limit_bytes=44 * 1024 * 1024
         ),
     )(chan_weights, freq_offsets, half_widths, beam_images)
 

time: 50 us -> 48.5 us (0.970)
  Pallas kernels: 47.3 us -> 45.3 us
  local copies, waits for them, and re-layouts: 2.52 us -> 3.02 us
    pallas_call x1, Pallas kernels: 47.3 us -> 45.3 us  [body(): pl.pallas_call(functools.partial(kernel, chans, slabs), out_shape=jax.Sha...]
    unnamed x1 -> x7, local copies, waits for them, and re-layouts: 2.52 us -> 3.02 us
where the time goes in v3:
time: 48.5 us; the launch traced here: 48.3 us
  Pallas kernels  45.3 us (93%)
  local copies, waits for them, and re-layouts  3.02 us (6%)
    pallas_call x1, Pallas kernels, body(): pl.pallas_call(functools.partial(kernel, chans, slabs), out_shape=jax.Sha...  45.3 us
    unnamed x7, local copies, waits for them, and re-layouts  3.02 us

profile of v3, /device:TPU:9, one launch (start us, length us, event | category | flops | bytes accessed | tf_op | source)
XLA Modules:
  0.0 48.3 jit_solution(9795238095603936842)
XLA Ops:
  0.0 0.0 copy-start
  0.0 0.7 %copy-done = s32[16]{0:T(128)S(1)} copy-done((s32[16]{0:T(128)S(1)}, s32[16]{0:T(128)}, u32[]{:S(2)}) %copy-start) | copy-done | bytes 88
  0.7 0.0 copy-start.1
  0.7 0.7 %copy-done.1 = f32[16]{0:T(128)S(1)} copy-done((f32[16]{0:T(128)S(1)}, f32[16]{0:T(128)}, u32[]{:S(2)}) %copy-start.1) | copy-done | bytes 88
  1.3 0.0 copy-start.2
  1.3 0.7 %copy-done.2 = s32[5]{0:T(128)S(1)} copy-done((s32[5]{0:T(128)S(1)}, s32[5]{0:T(128)}, u32[]{:S(2)}) %copy-start.2) | copy-done | bytes 44
  2.0 45.3 %shard_map.46 = f32[5,64,1024]{2,1,0:T(8,128)S(1)} custom-call(s32[16]{0:T(128)S(1)} %copy-done, f32[16]{0:T(128)S(1)} %copy-done.1, s32[5]{0:T(128)S(1)} %copy-done.2, f32[16,64,4096]{2,1,0:T(8,128)} %beam_ref.1), custom_call_target="tpu_custom_call" | custom-call | tf_op jit(solution)/shard_map/pallas_call | solution.py:326
  47.2 1.1 %copy.6 = f32[5,64,1024]{2,1,0:T(8,128)} copy(f32[5,64,1024]{2,1,0:T(8,128)S(1)} %shard_map.46) | data formatting | bytes 2621440
Async XLA Ops:
  0.0 0.7 %copy-start = (s32[16]{0:T(128)S(1)}, s32[16]{0:T(128)}, u32[]{:S(2)}) copy-start(s32[16]{0:T(128)} %w_ref.1) | copy-start | bytes 196
  0.7 0.7 %copy-start.1 = (f32[16]{0:T(128)S(1)}, f32[16]{0:T(128)}, u32[]{:S(2)}) copy-start(f32[16]{0:T(128)} %f_ref.1) | copy-start | bytes 196
  1.3 0.7 %copy-start.2 = (s32[5]{0:T(128)S(1)}, s32[5]{0:T(128)}, u32[]{:S(2)}) copy-start(s32[5]{0:T(128)} %h_ref.1) | copy-start | bytes 64
